TPU v7x, 512 devices: a whole 4x8x8 slice. The times are simulated.
512 devices in a mesh: roll: 64 (over z, y_lo, core), tensor: 8 (over x, y_hi).
Axes of the slice: x: 4, y: 8 (y_hi: 2, y_lo: 4; y = y_hi * 4 + y_lo), z: 8, core: 2. Of those that a mesh axis runs over, the one named last changes fastest.
Arguments:
- grad_out: bfloat16 [24576, 5120], P('roll', 'tensor'), may hold values from -6 to 6
- out_weight: bfloat16 [5120, 4096], P('roll', 'tensor'), may hold values from -0.078125 to 0.078125
- queries: bfloat16 [24576, 4096], P('roll', 'tensor'), may hold values from -6 to 6
- resp_key: bfloat16 [24576, 1024], P('roll', 'tensor'), may hold values from -5 to 5
- resp_value: bfloat16 [24576, 1024], P('roll', 'tensor'), may hold values from -5 to 5
- prefix_key: bfloat16 [256, 1024], P('roll', 'tensor'), may hold values from -5 to 5
- prefix_value: bfloat16 [256, 1024], P('roll', 'tensor'), may hold values from -5 to 5
- lengths: int32 [64], P('roll'), may hold values from 1 to 384
Outputs:
- grad_query: bfloat16 [24576, 4096], P('roll', 'tensor')
- grad_resp_key: bfloat16 [24576, 1024], P('roll', 'tensor')
- grad_resp_value: bfloat16 [24576, 1024], P('roll', 'tensor')
- grad_prefix_key: float32 [256, 1024], P('roll', 'tensor')
- grad_prefix_value: float32 [256, 1024], P('roll', 'tensor')
All inputs are finite; a program needn't handle non-finite values.
Results may differ from a plain program's by a relative error of at most 0.0063.
Values may be sent and summed in bfloat16 or wider, within the bound.
No kernel may reach another device: no remote copies, remote signals or barrier semaphores. Data moves between devices by JAX's collectives and lax.ppermute only.
A program may use at most 64 MiB of HBM per device.

v0:
```python
from functools import partial
import jax
import jax.numpy as jnp
from jax import lax
from jax.sharding import Mesh
from jax.sharding import PartitionSpec as P

HD = 128
ROWS = 384
ROLL = ("roll_0", "roll_1", "roll_2")


def in_order(parts, dim):
    parts = jnp.moveaxis(parts, 0, dim)
    shape = parts.shape
    return parts.reshape(*shape[:dim], shape[dim] * shape[dim + 1], *shape[dim + 2 :])


def stacked_from(x, axes, turns):
    parts = x[None]
    for k in turns:
        parts = lax.all_gather(parts, axes[k], axis=0, tiled=True)
    held = [lax.axis_size(axes[k]) for k in reversed(turns)]
    parts = parts.reshape(*held, *x.shape)
    turned = sorted(range(len(turns)), key=lambda place: turns[len(turns) - 1 - place])
    return parts.transpose(*turned, *range(len(turns), parts.ndim)).reshape(-1, *x.shape)


def gathered_by_axis(x, axes, turns, dim):
    return in_order(stacked_from(x, axes, turns), dim)


def side_by_side(arrays, axis, dim, along):
    widths = [a.shape[along] for a in arrays]
    both = jnp.concatenate(arrays, axis=along)
    whole = lax.all_gather(both, axis, axis=dim, tiled=True)
    return tuple(jnp.split(whole, [sum(widths[:k]) for k in range(1, len(widths))], axis=along))


def split_up(x, dim, length):
    before, after = (x.shape[:dim], x.shape[dim + 1 :])
    return jnp.moveaxis(x.reshape(*before, length, -1, *after), dim, 0)


def summed_on_arrival(x, axis, dim):
    length = lax.axis_size(axis)
    parts = lax.all_to_all(split_up(x, dim, length), axis, 0, 0, tiled=True)
    return jnp.sum(parts, axis=0)


def side_by_side_2(arrays, axis, dim, along):
    both = jnp.concatenate(arrays, axis=along)
    whole, at, done = (summed_on_arrival(both, axis, dim), 0, [])
    for a in arrays:
        done.append(lax.slice_in_dim(whole, at, at + a.shape[along], axis=along))
        at += a.shape[along]
    return tuple(done)


def block_terms(query_rows, grad_rows, offset, all_keys, all_values, prefix_rows, keep_prefix):
    row_count = query_rows.shape[0]
    local_heads = all_keys.shape[1] // HD
    group_size = query_rows.shape[1] // all_keys.shape[1]
    score_scale = HD ** (-0.5)
    query_heads = query_rows.reshape(row_count, local_heads, group_size, HD)
    grad_heads = grad_rows.reshape(row_count, local_heads, group_size, HD)
    key_heads = all_keys.reshape(-1, local_heads, HD)
    value_heads = all_values.reshape(-1, local_heads, HD)
    scores = (
        jnp.einsum("ikgd,jkd->kgij", query_heads, key_heads, preferred_element_type=jnp.float32)
        * score_scale
    )
    query_place = offset + jnp.arange(row_count, dtype=jnp.int32)[:, None]
    key_place = jnp.arange(key_heads.shape[0], dtype=jnp.int32)[None, :]
    allowed = (key_place < prefix_rows) | (key_place - prefix_rows <= query_place)
    scores = jnp.where(allowed, scores, -jnp.inf)
    row_max = jnp.max(scores, axis=-1, keepdims=True)
    shifted = jnp.exp(scores - row_max)
    row_total = jnp.sum(shifted, axis=-1, keepdims=True)
    soft_weights = shifted / row_total
    weights_low = soft_weights.astype(jnp.bfloat16)
    prob_grad = jnp.einsum(
        "ikgd,jkd->kgij", grad_heads, value_heads, preferred_element_type=jnp.float32
    )
    row_delta = jnp.sum(soft_weights * prob_grad, axis=-1, keepdims=True)
    score_low = (soft_weights * (prob_grad - row_delta) * score_scale).astype(jnp.bfloat16)
    query_grad = jnp.einsum(
        "kgij,jkd->ikgd", score_low, key_heads, preferred_element_type=jnp.float32
    )
    query_grad = query_grad.reshape(row_count, -1).astype(jnp.bfloat16)
    key_count = score_low.shape[-1]
    key_grad = jnp.einsum(
        "kgij,ikgd->jkd", score_low, query_heads, preferred_element_type=jnp.float32
    )
    value_grad = jnp.einsum(
        "kgij,ikgd->jkd", weights_low, grad_heads, preferred_element_type=jnp.float32
    )
    return (
        query_grad,
        key_grad.reshape(key_count, -1),
        value_grad.reshape(key_count, -1),
        row_max,
        row_total,
        row_delta,
    )


def body(grad_out, out_weight, queries, resp_key, resp_value, prefix_key, prefix_value, lengths):
    rows_here = queries.shape[0]
    responses = rows_here // ROWS
    full_grad = lax.all_gather(grad_out, "tensor", axis=1, tiled=True)
    projected = jnp.dot(
        full_grad,
        gathered_by_axis(out_weight, ROLL, (1, 0, 2), 0),
        preferred_element_type=jnp.float32,
    )
    position = jnp.arange(rows_here, dtype=jnp.int32)
    matches = (position // ROWS)[:, None] == jnp.arange(responses, dtype=jnp.int32)[None, :]
    row_limit = jnp.sum(jnp.where(matches, lengths[None, :], 0), axis=1)
    valid_rows = (position % ROWS < row_limit).astype(jnp.float32)
    out_grad = (projected * valid_rows[:, None]).astype(jnp.bfloat16)
    prefix_keys, prefix_values = side_by_side((prefix_key, prefix_value), ROLL, 0, 1)
    prefix_rows = prefix_keys.shape[0]
    key_width = prefix_key.shape[1]
    block_rows = min(128, ROWS)
    query_parts, key_parts, value_parts, saved = ([], [], [], [])
    all_keys = jnp.concatenate([prefix_keys, resp_key], axis=0)
    all_values = jnp.concatenate([prefix_values, resp_value], axis=0)
    key_rows = all_keys.shape[0]
    key_sum = jnp.zeros((key_rows, key_width), jnp.float32)
    value_sum = jnp.zeros((key_rows, key_width), jnp.float32)
    for part_index in range(ROWS // block_rows):
        offset = part_index * block_rows
        compute_block = partial(
            block_terms,
            queries[offset : offset + block_rows],
            out_grad[offset : offset + block_rows],
            offset,
            all_keys,
            all_values,
            prefix_rows,
            True,
        )
        result = compute_block()
        query_grad, key_grad, value_grad, row_max, row_total, row_delta = result
        query_parts.append(query_grad)
        key_sum = key_sum + key_grad
        value_sum = value_sum + value_grad
        saved.append((0, offset, offset, row_max, row_total, row_delta))
    prefix_key_sum = key_sum[:prefix_rows]
    prefix_value_sum = value_sum[:prefix_rows]
    key_sum = key_sum[prefix_rows:]
    value_sum = value_sum[prefix_rows:]
    key_parts.append(key_sum.astype(jnp.bfloat16))
    value_parts.append(value_sum.astype(jnp.bfloat16))
    grad_prefix_key, grad_prefix_value = side_by_side_2(
        (prefix_key_sum, prefix_value_sum), ROLL, 0, 1
    )
    grad_query = jnp.concatenate(query_parts, axis=0)
    grad_resp_key = key_parts[0]
    grad_resp_value = value_parts[0]
    return (grad_query, grad_resp_key, grad_resp_value, grad_prefix_key, grad_prefix_value)


def solution(mesh):
    torus = Mesh(
        mesh.devices.reshape(8, 4, 2, mesh.shape["tensor"]),
        ("roll_0", "roll_1", "roll_2", "tensor"),
    )
    placed = (
        P(ROLL, "tensor"),
        P(ROLL, "tensor"),
        P(ROLL, "tensor"),
        P(ROLL, "tensor"),
        P(ROLL, "tensor"),
        P(ROLL, "tensor"),
        P(ROLL, "tensor"),
        P(ROLL),
    )
    return jax.shard_map(
        body,
        mesh=torus,
        in_specs=placed,
        out_specs=(
            P(ROLL, "tensor"),
            P(ROLL, "tensor"),
            P(ROLL, "tensor"),
            P(ROLL, "tensor"),
            P(ROLL, "tensor"),
        ),
        check_vma=False,
    )
```

profile of v0, /device:TPU:1, one launch (start us, length us, event | category | flops | bytes accessed | tf_op | source)
XLA Modules:
  0.0 262.5 jit_solution(3908151491509216259)
XLA Ops:
  7.2 0.0 all-gather.8.cloned.1.call-start
  7.2 14.7 %all-gather = bf16[320,512]{1,0:T(8,128)(2,1)} all-gather(bf16[80,512]{1,0:T(8,128)(2,1)} %param.9), channel_id=2, replica_groups=mesh['roll_0'=8,'roll_1'=4,'roll_2'=2,'tensor'=8] {'roll_1'}, dimensions={0}, use_global_device_ids=true | all-gather | bytes 409600 | tf_op jit(solution)/shard_map/all_gather | solution.py:22
  21.9 0.0 all-gather.8.cloned.1.call-update
  21.9 0.0 all-gather.10.cloned.1.call-start
  21.9 48.3 %all-gather.8.cloned.1.call-done = bf16[32,80,512]{2,1,0:T(8,128)(2,1)} async-done(((bf16[4,80,512]{2,1,0:T(8,128)(2,1)}), bf16[32,80,512]{2,1,0:T(8,128)(2,1)}) %all-gather.8.cloned.1.call-update) | async-done | bytes 2621456 | tf_op jit(solution)/shard_map/all_gather | solution.py:22
  70.3 0.0 all-gather.10.cloned.1.call-update
  70.3 0.0 all-gather.6.cloned.1.call-start
  70.4 0.7 all-gather.6.cloned.1.call-update
  71.1 83.0 %all-gather.1 = bf16[64,4,256]{2,1,0:T(4,128)(2,1)S(1)} all-gather(bf16[1,4,256]{2,1,0:T(4,128)(2,1)S(1)} %maximum_bitcast_fusion.5), channel_id=1, replica_groups=mesh['roll_0'=8,'roll_1'=4,'roll_2'=2,'tensor'=8] {'roll_0','roll_1','ro..., dimensions={0}, use_global_device_ids=true | all-gather | bytes 133120 | tf_op jit(solution)/shard_map/all_gather | solution.py:36
  154.1 0.1 copy.150
  154.9 0.1 copy.151
  155.0 0.1 copy.149
  155.2 0.2 fusion.27
  155.5 0.3 fusion.44
  155.8 0.2 fusion.15
  156.0 0.3 fusion.43
  156.4 0.5 copy-done.2
  156.9 0.2 fusion.17
  157.1 0.3 fusion.45
  157.4 0.2 fusion.13
  157.6 0.0 all-gather.10.cloned.1.call-done
  157.6 5.3 %copy.102 = bf16[8,4,2,80,512]{4,3,2,1,0:T(8,128)(2,1)} copy(bf16[8,4,2,80,512]{4,3,1,0,2:T(8,128)(2,1)} %bitcast.153) | data formatting | bytes 10485760 | tf_op jit(solution)/shard_map/transpose | solution.py:26
  163.0 42.9 %all-gather.6.cloned.1.call-done = bf16[384,5120]{1,0:T(8,128)(2,1)} async-done(((bf16[384,640]{1,0:T(8,128)(2,1)}), bf16[384,5120]{1,0:T(8,128)(2,1)}) %all-gather.6.cloned.1.call-update) | async-done | bytes 3932176 | tf_op jit(solution)/shard_map/all_gather | solution.py:111
  205.9 5.9 %fusion.6 = bf16[384,512]{1,0:T(8,128)(2,1)S(1)} fusion(bf16[384,5120]{1,0:T(8,128)(2,1)} %all-gather.6.cloned.1.call-done, bf16[5120,512]{1,0:T(8,128)(2,1)} %bitcast.154, f32[384]{0:T(512)S(1)} %fusion.31), kind=kOutput, calls=%fused_computation.22 | convolution fusion | flops 2013659136 | bytes 9569792 | tf_op jit(solution)/shard_map/dot_general | solution.py:112
  211.7 0.7 fusion.40
  212.4 1.7 copy.153
  214.1 0.8 copy.154
  214.8 2.5 convolution_bitcast_fusion.4
  217.4 1.1 convolution_bitcast_fusion.3
  218.5 0.2 copy-done.3
  218.7 0.0 copy-done.10
  218.7 0.1 copy-done.13
  218.8 1.4 multiply_reduce_fusion.1
  220.2 1.4 multiply_reduce_fusion
  221.6 0.1 copy.152
  221.7 0.3 multiply_reduce_fusion.2
  222.1 0.6 copy-done.14
  222.7 0.1 copy-done.15
  222.8 0.4 fusion.11
  223.2 0.9 copy-done.4
  224.1 0.4 copy-done.6
  224.5 0.4 fusion.19
  224.9 0.3 convolution_bitcast_fusion.7
  225.2 0.6 copy-done.1
  225.8 0.4 copy-done.5
  226.2 0.4 fusion.20
  226.6 0.3 convolution_bitcast_fusion.6
  226.9 0.4 fusion.18
  227.3 0.3 fusion.8
  227.7 0.3 convolution_convert_fusion.2
  228.0 0.1 copy.128
  228.1 0.8 reshape.248
  228.9 12.9 %all-to-all-start = ((f32[64,4,256]{2,1,0:T(4,128)}), f32[64,4,256]{2,1,0:T(4,128)S(1)}, u32[]{:S(2)}, u32[]{:S(2)}) async-start(f32[64,4,256]{2,1,0:T(4,128)} %reshape.248), calls=%async_computation | async-start | bytes 524288 | tf_op jit(solution)/shard_map/all_to_all | solution.py:47
  241.8 0.8 copy.130
  242.6 0.8 copy.129
  243.3 0.1 copy.116
  243.5 0.3 convolution_convert_fusion.1
  243.8 0.1 copy.117
  243.9 0.3 convolution_convert_fusion
  244.2 0.1 copy.118
  244.3 0.8 pad_maximum_fusion
  245.1 10.3 %all-to-all-done = f32[64,4,256]{2,1,0:T(4,128)S(1)} async-done(((f32[64,4,256]{2,1,0:T(4,128)}), f32[64,4,256]{2,1,0:T(4,128)S(1)}, u32[]{:S(2)}, u32[]{:S(2)}) %all-to-all-start) | async-done | bytes 262176 | tf_op jit(solution)/shard_map/all_to_all | solution.py:47
  255.3 0.1 reduce_sum.73
  255.4 0.6 fusion.42
  (35 shorter events, 0.2 us)
Async XLA Ops:
  7.2 63.1 %all-gather.8.cloned.1.call-start = ((), (), s32[]{:S(2)}) async-start(), calls=%async_computation.2 | async-start | bytes 2949120 | tf_op jit(solution)/shard_map/all_gather | solution.py:22
  21.9 135.7 %all-gather.10.cloned.1.call-start = ((), (), s32[]{:S(2)}) async-start(), calls=%async_computation.3 | async-start | bytes 7864320 | tf_op jit(solution)/shard_map/all_gather | solution.py:22
  70.3 0.8 copy-start.11
  70.3 0.8 copy-start.12
  70.3 83.8 %copy-start.8 = (bf16[384,512]{1,0:T(8,128)(2,1)S(1)}, bf16[384,512]{1,0:T(8,128)(2,1)}, u32[]{:S(2)}) copy-start(bf16[384,512]{1,0:T(8,128)(2,1)} %param.10) | copy-start | bytes 1179652
  70.3 135.6 %all-gather.6.cloned.1.call-start = ((), (), s32[]{:S(2)}) async-start(), calls=%async_computation.1 | async-start | bytes 4423680 | tf_op jit(solution)/shard_map/all_gather | solution.py:111
  71.1 84.4 %copy-start.7 = (bf16[384,128]{1,0:T(8,128)(2,1)S(1)}, bf16[384,128]{1,0:T(8,128)(2,1)}, u32[]{:S(2)}) copy-start(bf16[384,128]{1,0:T(8,128)(2,1)} %param.11) | copy-start | bytes 294916
  155.8 1.1 copy-start.2
  156.9 63.3 %copy-start = (f32[1,4,128,640]{2,3,1,0:T(8,128)}, f32[1,4,128,640]{2,3,1,0:T(8,128)S(1)}, u32[]{:S(2)}) copy-start(f32[1,4,128,640]{2,3,1,0:T(8,128)S(1)} %get-tuple-element.39) | copy-start | bytes 3932164
  214.8 2.6 copy-start.9
  217.4 1.3 copy-start.3
  217.4 1.3 copy-start.10
  217.4 1.4 copy-start.13
  221.7 1.0 copy-start.14
  221.7 1.1 copy-start.15
  222.8 1.3 copy-start.4
  222.8 1.7 copy-start.6
  224.5 1.3 copy-start.1
  224.5 1.7 copy-start.5
  228.9 26.4 %all-to-all-start = ((f32[64,4,256]{2,1,0:T(4,128)}), f32[64,4,256]{2,1,0:T(4,128)S(1)}, u32[]{:S(2)}, u32[]{:S(2)}) async-start(f32[64,4,256]{2,1,0:T(4,128)} %reshape.248), calls=%async_computation | async-start | bytes 524288 | tf_op jit(solution)/shard_map/all_to_all | solution.py:47
Sparse Core Ops, SparseCore 0:
  22.0 48.2 all-gather.7
  72.4 26.1 all-gather.9
  101.7 104.0 all-gather.5
where the time goes:
time: 263 us
  waiting for transfers between devices  102 us (39%)
  blocking collectives  97.6 us (37%)
  local copies, waits for them, and re-layouts  16.2 us (6%)
  matrix products  16 us (6%)
  between operations  14.7 us (6%)
  starting transfers between devices  13 us (5%)
  other arithmetic  2.8 us (1%)
    all_gather x1, blocking collectives, side_by_side(): whole = lax.all_gather(both, axis, axis=dim, tiled=True)  83 us
    all_gather x2, waiting for transfers between devices, stacked_from(): parts = lax.all_gather(parts, axes[k], axis=0, tiled=True)  48.3 us
    all_gather x1, waiting for transfers between devices, body(): full_grad = lax.all_gather(grad_out, 'tensor', axis=1, tiled=True)  42.9 us
    all_gather x1, blocking collectives, stacked_from(): parts = lax.all_gather(parts, axes[k], axis=0, tiled=True)  14.7 us
    all_to_all x1, starting transfers between devices, summed_on_arrival(): parts = lax.all_to_all(split_up(x, dim, length), axis, 0, 0, tiled=True)  12.9 us
    all_to_all x1, waiting for transfers between devices, summed_on_arrival(): parts = lax.all_to_all(split_up(x, dim, length), axis, 0, 0, tiled=True)  10.3 us
    dot_general x1, matrix products, body(): jnp.dot(full_grad, gathered_by_axis(out_weight, ROLL, (1, 0, 2), 0), pref...  5.87 us
    unnamed x38, local copies, waits for them, and re-layouts  5.72 us
  transfers between devices with their start and end apart: 4, of which 3 were waited for; matrix products, arithmetic and copies ran while one was open for 4% of the time, Pallas kernels for 0%

commit v1 on v0

--- a/solution.py
+++ b/solution.py
@@ -19,7 +19,15 @@
 def stacked_from(x, axes, turns):
     parts = x[None]
     for k in turns:
-        parts = lax.all_gather(parts, axes[k], axis=0, tiled=True)
+
+        def lay_ratios_on_mesh(local_x, along_axis):
+            e_now = lax.axis_size(along_axis)
+            block_now = jnp.stack([local_x] * e_now, 0)
+            newest = lax.all_to_all(block_now, along_axis, 0, 0)
+            piece_next = jnp.concatenate(newest, 0)
+            return piece_next
+
+        parts = lay_ratios_on_mesh(parts, axes[k])
     held = [lax.axis_size(axes[k]) for k in reversed(turns)]
     parts = parts.reshape(*held, *x.shape)
     turned = sorted(range(len(turns)), key=lambda place: turns[len(turns) - 1 - place])

time: 263 us -> 195 us (0.74)
  the two profiles are of different devices: /device:TPU:1 before, /device:TPU:58 now
where the time goes in v1:
time: 195 us; the launch traced here: 194 us
  blocking collectives  118 us (61%)
  starting transfers between devices  21.4 us (11%)
  local copies, waits for them, and re-layouts  15.6 us (8%)
  between operations  15.1 us (8%)
  matrix products  11.8 us (6%)
  waiting for transfers between devices  9.46 us (5%)
  other arithmetic  3.25 us (2%)
    all_gather x1, blocking collectives, side_by_side(): whole = lax.all_gather(both, axis, axis=dim, tiled=True)  96.2 us
    all_to_all x2, blocking collectives, lay_ratios_on_mesh(): newest = lax.all_to_all(block_now, along_axis, 0, 0)  21.4 us
    all_to_all x1, starting transfers between devices, summed_on_arrival(): parts = lax.all_to_all(split_up(x, dim, length), axis, 0, 0, tiled=True)  10.9 us
    all_to_all x1, starting transfers between devices, lay_ratios_on_mesh(): newest = lax.all_to_all(block_now, along_axis, 0, 0)  10.4 us
    all_to_all x1, waiting for transfers between devices, summed_on_arrival(): parts = lax.all_to_all(split_up(x, dim, length), axis, 0, 0, tiled=True)  8.78 us
    unnamed x26, local copies, waits for them, and re-layouts  7.09 us
    dot_general x1, matrix products, body(): jnp.dot(full_grad, gathered_by_axis(out_weight, ROLL, (1, 0, 2), 0), pref...  6.68 us
  transfers between devices with their start and end apart: 3, of which 1 were waited for; matrix products, arithmetic and copies ran while one was open for 6% of the time, Pallas kernels for 0%

profile of v1, /device:TPU:58, one launch (start us, length us, event | category | flops | bytes accessed | tf_op | source)
XLA Modules:
  0.0 194.3 jit_solution(10011941818483352851)
XLA Ops:
  7.2 0.0 all-gather.3.cloned.1.call-start
  7.2 0.7 all-gather.3.cloned.1.call-update
  7.9 0.9 stack.9
  8.8 13.5 %all_to_all.20 = bf16[4,1,80,512]{3,2,1,0:T(8,128)(2,1)S(1)} all-to-all(bf16[4,1,80,512]{3,2,1,0:T(8,128)(2,1)S(1)} %stack.9), channel_id=1, replica_groups=mesh['roll_0'=8,'roll_1'=4,'roll_2'=2,'tensor'=8] {'roll_1'}, dimensions={0} | all-to-all | bytes 655360 | tf_op jit(solution)/shard_map/all_to_all | solution.py:26
  22.3 1.8 stack.10
  24.1 10.4 %all-to-all-start.1 = ((bf16[8,4,80,512]{3,2,1,0:T(8,128)(2,1)}), bf16[8,4,80,512]{3,2,1,0:T(8,128)(2,1)S(1)}, u32[]{:S(2)}, u32[]{:S(2)}) async-start(bf16[8,4,80,512]{3,2,1,0:T(8,128)(2,1)} %stack.10), calls=%async_computation.1 | async-start | bytes 5242880 | tf_op jit(solution)/shard_map/all_to_all | solution.py:26
  34.6 0.0 copy-done.7
  34.6 0.0 copy-done.8
  34.6 0.0 copy-start.6
  34.6 96.2 %all-gather = bf16[64,4,256]{2,1,0:T(4,128)(2,1)S(1)} all-gather(bf16[1,4,256]{2,1,0:T(4,128)(2,1)S(1)} %maximum_bitcast_fusion.5), channel_id=1, replica_groups=mesh['roll_0'=8,'roll_1'=4,'roll_2'=2,'tensor'=8] {'roll_0','roll_1','ro..., dimensions={0}, use_global_device_ids=true | all-gather | bytes 133120 | tf_op jit(solution)/shard_map/all_gather | solution.py:44
  130.9 1.1 fusion.40
  131.9 0.1 copy.113
  132.7 0.1 copy.114
  132.8 0.1 copy.112
  133.0 0.2 fusion.28
  133.3 0.0 copy-done.6
  133.3 0.3 fusion.45
  133.6 0.0 copy-start.4
  133.6 0.2 fusion.16
  133.8 0.9 copy-done.4
  134.7 0.3 fusion.44
  135.0 0.0 copy-start.2
  135.0 0.2 fusion.18
  135.2 0.9 copy-done.2
  136.1 0.3 fusion.46
  136.4 1.1 copy-done
  137.5 0.2 fusion.14
  137.7 0.0 all-to-all-done.1
  137.7 0.5 pad_maximum_fusion
  138.2 7.9 %all_to_all.21 = bf16[2,32,80,512]{3,2,1,0:T(8,128)(2,1)S(1)} all-to-all(bf16[2,32,80,512]{3,2,1,0:T(8,128)(2,1)S(1)} %pad_maximum_fusion), channel_id=1, replica_groups=mesh['roll_0'=8,'roll_1'=4,'roll_2'=2,'tensor'=8] {'roll_2'}, dimensions={0} | all-to-all | bytes 10485760 | tf_op jit(solution)/shard_map/all_to_all | solution.py:26
  146.1 2.8 %copy.65 = bf16[2,32,80,512]{3,2,0,1:T(8,128)(2,1)} copy(bf16[2,32,80,512]{3,2,1,0:T(8,128)(2,1)S(1)} %all_to_all.21) | data formatting | bytes 10485760 | tf_op jit(solution)/shard_map/all_to_all | solution.py:26
  149.0 6.7 %fusion.7 = bf16[384,512]{0,1:T(8,128)(2,1)S(1)} fusion(bf16[5120,512]{1,0:T(8,128)(2,1)} %bitcast.158, bf16[384,5120]{1,0:T(8,128)(2,1)} %all-gather.3.cloned.1.call-done, f32[384]{0:T(512)S(1)} %fusion.32), kind=kOutput, calls=%fused_computation.24 | convolution fusion | flops 2013659136 | bytes 9569792 | tf_op jit(solution)/shard_map/dot_general | solution.py:120
  155.6 0.1 fusion.41
  155.7 0.4 convolution_bitcast_fusion.4
  156.1 0.9 copy-done.3
  157.1 0.4 convolution_bitcast_fusion.3
  157.4 0.5 copy-done.9
  157.9 0.4 multiply_reduce_fusion.1
  158.3 0.0 copy-start.1
  158.3 0.4 multiply_reduce_fusion
  158.7 0.9 copy-done.1
  159.6 0.4 multiply_reduce_fusion.2
  160.0 0.4 fusion.12
  160.4 0.4 fusion.20
  160.8 0.3 convolution_bitcast_fusion.7
  161.1 0.4 fusion.21
  161.5 0.3 convolution_bitcast_fusion.6
  161.8 0.4 fusion.19
  162.2 0.3 fusion.9
  162.6 0.3 convolution_convert_fusion.2
  162.9 0.1 copy.88
  163.1 0.8 reshape.248
  163.8 10.9 %all-to-all-start.3 = ((f32[64,4,256]{2,1,0:T(4,128)}), f32[64,4,256]{2,1,0:T(4,128)S(1)}, u32[]{:S(2)}, u32[]{:S(2)}) async-start(f32[64,4,256]{2,1,0:T(4,128)} %reshape.248), calls=%async_computation.3 | async-start | bytes 524288 | tf_op jit(solution)/shard_map/all_to_all | solution.py:55
  174.7 0.8 copy.90
  175.5 0.8 copy.89
  176.2 0.1 copy.79
  176.3 0.3 convolution_convert_fusion.1
  176.6 0.1 copy.80
  176.8 0.3 convolution_convert_fusion
  177.1 0.1 copy.81
  177.2 0.8 pad_maximum_fusion.1
  178.0 8.8 %all-to-all-done.3 = f32[64,4,256]{2,1,0:T(4,128)S(1)} async-done(((f32[64,4,256]{2,1,0:T(4,128)}), f32[64,4,256]{2,1,0:T(4,128)S(1)}, u32[]{:S(2)}, u32[]{:S(2)}) %all-to-all-start.3) | async-done | bytes 262176 | tf_op jit(solution)/shard_map/all_to_all | solution.py:55
  186.7 0.1 reduce_sum.73
  186.8 0.6 fusion.43
  (20 shorter events, 0.2 us)
Async XLA Ops:
  7.2 141.8 %all-gather.3.cloned.1.call-start = ((), (), s32[]{:S(2)}) async-start(), calls=%async_computation.4 | async-start | bytes 4423680 | tf_op jit(solution)/shard_map/all_gather | solution.py:119
  24.1 10.5 %copy-start.7 = (bf16[4,128]{1,0:T(4,128)(2,1)S(1)}, bf16[4,128]{1,0:T(4,128)(2,1)}, u32[]{:S(2)}) copy-start(bf16[4,128]{1,0:T(4,128)(2,1)} %param.14) | copy-start | bytes 3076
  24.1 10.5 %copy-start.8 = (bf16[4,128]{1,0:T(4,128)(2,1)S(1)}, bf16[4,128]{1,0:T(4,128)(2,1)}, u32[]{:S(2)}) copy-start(bf16[4,128]{1,0:T(4,128)(2,1)} %param.13) | copy-start | bytes 3076
  24.1 113.6 %all-to-all-start.1 = ((bf16[8,4,80,512]{3,2,1,0:T(8,128)(2,1)}), bf16[8,4,80,512]{3,2,1,0:T(8,128)(2,1)S(1)}, u32[]{:S(2)}, u32[]{:S(2)}) async-start(bf16[8,4,80,512]{3,2,1,0:T(8,128)(2,1)} %stack.10), calls=%async_computation.1 | async-start | bytes 5242880 | tf_op jit(solution)/shard_map/all_to_all | solution.py:26
  34.6 98.7 %copy-start.6 = (bf16[384,128]{1,0:T(8,128)(2,1)S(1)}, bf16[384,128]{1,0:T(8,128)(2,1)}, u32[]{:S(2)}) copy-start(bf16[384,128]{1,0:T(8,128)(2,1)} %param.11) | copy-start | bytes 294916
  133.6 1.1 copy-start.4
  135.0 1.1 copy-start.2
  136.4 1.1 copy-start
  149.0 6.8 %copy-start.5 = (f32[1,4,128,640]{2,3,1,0:T(8,128)S(1)}, f32[1,4,128,640]{2,3,1,0:T(8,128)}, u32[]{:S(2)}) copy-start(f32[1,4,128,640]{2,3,1,0:T(8,128)} %copy-done.4) | copy-start | bytes 3932164
  155.7 1.3 copy-start.3
  157.0 0.9 copy-start.9
  158.3 1.3 copy-start.1
  163.8 22.9 %all-to-all-start.3 = ((f32[64,4,256]{2,1,0:T(4,128)}), f32[64,4,256]{2,1,0:T(4,128)S(1)}, u32[]{:S(2)}, u32[]{:S(2)}) async-start(f32[64,4,256]{2,1,0:T(4,128)} %reshape.248), calls=%async_computation.3 | async-start | bytes 524288 | tf_op jit(solution)/shard_map/all_to_all | solution.py:55
Sparse Core Ops, SparseCore 0:
  11.2 102.4 all-gather.2
